TPU v7x, 128 devices: a whole 4x4x4 slice. The times are simulated.
128 devices in a mesh: rep: 2 (over z_hi), shard: 64 (over y, z_lo, x, core).
Axes of the slice: x: 4, y: 4, z: 4 (z_hi: 2, z_lo: 2; z = z_hi * 2 + z_lo), core: 2. Of those that a mesh axis runs over, the one named last changes fastest.
Arguments:
- dense: bfloat16 [32768, 128], P(('rep', 'shard')), may hold values from -6 to 6
- small_ids: int32 [32768, 32], P(('rep', 'shard')), may hold values from 0 to 511
- labels: int32 [32768], P(('rep', 'shard')), may hold values 0 or 1
- small_tables: bfloat16 [32, 512, 128], replicated, may hold values from -6 to 6
- large_tables: bfloat16 [64, 8192, 128], P('shard'), may hold values from -6 to 6
- batch_sizes: int32 [64, 128], replicated, may hold values from 1 to 128, as said below
- bag_ends: int32 [64, 128, 128], P('shard'), may hold values from 0 to 256, as said below
- owner_row_index: int32 [64, 128, 256], P('shard'), may hold values from 0 to 8191
- w_first: bfloat16 [4784, 1024], replicated, may hold values from -0.09375 to 0.09375
- b_first: float32 [1024], replicated, may hold values from -3 to 3
- w_out: float32 [1024], replicated, may hold values from -0.1875 to 0.1875
Outputs:
- small_new: bfloat16 [32, 512, 128], replicated
- large_new: bfloat16 [64, 8192, 128], P('shard')
Inputs may be any that keep to these rules, and one draw needn't show every extreme that they name: `batch_sizes`: every feature has some owner, and every owner some feature, with exactly 128. `bag_ends`: nondecreasing along the last dimension; bags j >= batch_sizes[f, d] are empty; some bag list reaches 256.
All inputs are finite; a program needn't handle non-finite values. No bound on the sum of `labels` on one device may be relied on, other than what follows from the above.
Results may differ from a plain program's by a relative error of at most 0.0095.
Values may be sent and summed in bfloat16 or wider, within the bound.
A program may use at most 192 MiB of HBM per device.

v0:
```python
import jax
import jax.numpy as jnp
from jax import lax
from jax.sharding import PartitionSpec as P

step_size = 32.0


def as_sent(array):

    def short(part):
        return part.astype(jnp.bfloat16) if part.dtype == jnp.float32 else part

    return jax.tree.map(short, array)


def gathered_total(array, axis):
    return lax.all_gather(array, axis).astype(jnp.float32).sum(0)


def bag_members(limits, slot_total):
    starts = jnp.concatenate(
        [jnp.zeros(limits.shape[:-1] + (1,), jnp.int32), limits[..., :-1]], axis=-1
    )
    positions = jnp.arange(slot_total, dtype=jnp.int32)
    inside = (positions >= starts[..., None]) & (positions < limits[..., None])
    return inside.astype(jnp.bfloat16)


def silu_slope(preacts):
    squash = jax.nn.sigmoid(preacts)
    return squash * (1.0 + preacts * (1.0 - squash))


def spread_table(size_table, batch_rows, bag_span):
    chosen = jnp.arange(batch_rows, dtype=jnp.int32) * size_table[..., None] // batch_rows
    return (chosen[..., None] == jnp.arange(bag_span, dtype=jnp.int32)).astype(jnp.bfloat16)


def take_rows(table_one, row_list):
    return table_one[row_list]


def lower_pairs(gram_matrix, vec_count):
    pieces = [gram_matrix[:, index, :index] for index in range(1, vec_count)]
    return jnp.concatenate(pieces, axis=1)


def lower_square(pair_grad, vec_count):
    rows_list = []
    offset = 0
    for index in range(vec_count):
        piece = pair_grad[:, offset : offset + index]
        offset = offset + index
        rows_list.append(jnp.pad(piece, ((0, 0), (0, vec_count - index))))
    return jnp.stack(rows_list, axis=1)


def table_grads(row_list, members, gradient_list, row_total):
    slot_vectors = jnp.einsum(
        "fdks,fdke->fdse", members, gradient_list, preferred_element_type=jnp.float32
    )
    embed_width = gradient_list.shape[-1]

    def one_table(values, row_index):
        return jax.ops.segment_sum(
            values.reshape(-1, embed_width), row_index.reshape(-1), row_total
        )

    return jax.vmap(one_table)(slot_vectors, row_list)


def shards(
    dense,
    small_ids,
    labels,
    small_tables,
    large_tables,
    batch_sizes,
    bag_ends,
    owner_row_index,
    w_first,
    b_first,
    w_out,
):
    groups = lax.axis_size("shard")
    replica = lax.axis_index("rep")
    member_id = lax.axis_index("shard")
    batch_rows, embed_width = dense.shape
    owned_tables, embedding_rows = (large_tables.shape[0], large_tables.shape[1])
    small_count, small_rows = (small_tables.shape[0], small_tables.shape[1])
    feat_count = batch_sizes.shape[0]
    bag_span = bag_ends.shape[2]
    slot_total = owner_row_index.shape[2]
    pair_count = w_first.shape[0] - embed_width
    vec_count = 1 + small_count + feat_count
    first_dest = replica * groups
    own_limits = lax.dynamic_slice_in_dim(bag_ends, first_dest, groups, 1)
    own_rows = lax.dynamic_slice_in_dim(owner_row_index, first_dest, groups, 1)
    recv_sizes = lax.dynamic_slice_in_dim(batch_sizes, first_dest + member_id, 1, 1)[:, 0]
    members = bag_members(own_limits, slot_total)
    collected_rows = jax.vmap(take_rows)(large_tables, own_rows)
    pooled = jnp.einsum(
        "fdks,fdse->fdke", members, collected_rows, preferred_element_type=jnp.float32
    ).astype(jnp.bfloat16)
    arrived = lax.all_to_all(pooled, "shard", split_axis=1, concat_axis=0, tiled=True)
    recv_spread = spread_table(recv_sizes, batch_rows, bag_span)
    large_feat = jnp.einsum(
        "fbj,fje->bfe", recv_spread, arrived[:, 0], preferred_element_type=jnp.float32
    ).astype(jnp.bfloat16)
    small_hot = (small_ids[:, :, None] == jnp.arange(small_rows, dtype=jnp.int32)).astype(
        jnp.bfloat16
    )
    minor_feature = jnp.einsum(
        "btr,tre->bte", small_hot, small_tables, preferred_element_type=jnp.float32
    ).astype(jnp.bfloat16)
    vectors = jnp.concatenate([dense[:, None, :], minor_feature, large_feat], axis=1)
    gram_matrix = jnp.einsum("bie,bje->bij", vectors, vectors, preferred_element_type=jnp.float32)
    pair_values = (lower_pairs(gram_matrix, vec_count) * embed_width ** (-0.5)).astype(jnp.bfloat16)
    features = jnp.concatenate([pair_values, dense], axis=1)
    preact = jnp.dot(features, w_first, preferred_element_type=jnp.float32) + b_first
    hidden = jax.nn.silu(preact)
    logits = jnp.sum(hidden * w_out[None, :], axis=1)
    logit_grad = jax.nn.sigmoid(logits) - labels.astype(jnp.float32)
    pre_grad = (logit_grad[:, None] * w_out[None, :] * silu_slope(preact)).astype(jnp.bfloat16)
    pair_grad = jnp.einsum(
        "bh,ph->bp", pre_grad, w_first[:pair_count], preferred_element_type=jnp.float32
    ) * embed_width ** (-0.5)
    lower_part = lower_square(pair_grad, vec_count)
    symmetric = lower_part + jnp.swapaxes(lower_part, 1, 2)
    vec_grad = jnp.einsum("bij,bje->bie", symmetric, vectors.astype(jnp.float32)).astype(
        jnp.bfloat16
    )
    small_local = jnp.einsum(
        "btr,bte->tre",
        small_hot,
        vec_grad[:, 1 : 1 + small_count],
        preferred_element_type=jnp.float32,
    )
    small_sum = lax.psum(small_local, ("rep", "shard"))
    small_new = (small_tables.astype(jnp.float32) - step_size * small_sum).astype(jnp.bfloat16)
    large_grad_part = vec_grad[:, 1 + small_count :]
    folded = jnp.einsum(
        "fbj,bfe->fje", recv_spread, large_grad_part, preferred_element_type=jnp.float32
    ).astype(jnp.bfloat16)
    accumulate_gradient = lax.all_to_all(
        folded[:, None], "shard", split_axis=0, concat_axis=1, tiled=True
    )
    local_grad = table_grads(own_rows, members, accumulate_gradient, embedding_rows)
    large_grad = jax.tree.map(
        lambda part: part.astype(jnp.float32),
        jax.tree.map(lambda part: gathered_total(part, "rep"), as_sent(local_grad)),
    )
    large_new = (large_tables.astype(jnp.float32) - step_size * large_grad).astype(jnp.bfloat16)
    return (small_new, large_new)


def solution(mesh):
    placed = (
        P(("rep", "shard"), None),
        P(("rep", "shard"), None),
        P(("rep", "shard")),
        P(),
        P("shard", None, None),
        P(),
        P("shard", None, None),
        P("shard", None, None),
        P(),
        P(),
        P(),
    )
    return jax.shard_map(
        shards, mesh=mesh, in_specs=placed, out_specs=(P(), P("shard", None, None)), check_vma=False
    )
```

profile of v0, /device:TPU:1, one launch (start us, length us, event | category | flops | bytes accessed | tf_op | source)
XLA Modules:
  0.0 922.3 jit_solution(10983050159655116990)
XLA Ops:
  11.2 266.0 %gather_fusion = bf16[16384,128]{1,0:T(8,128)(2,1)} fusion(bf16[1,8192,128]{2,1,0:T(8,128)(2,1)} %param.15, s32[16384]{0:T(1024)S(1)} %bitcast.526), kind=kCustom, calls=%fused_computation | custom fusion | bytes 8519680 | tf_op jit(solution)/shard_map/vmap()/gather | solution.py:41
  277.2 6.3 convert_bitcast_fusion.2
  283.5 11.1 %all-to-all-start = ((bf16[1,64,128,128]{3,2,0,1:T(8,128)(2,1)}), bf16[1,64,128,128]{3,2,0,1:T(8,128)(2,1)S(1)}, u32[]{:S(2)}, u32[]{:S(2)}) async-start(bf16[1,64,128,128]{3,2,0,1:T(8,128)(2,1)} %convert_bitcast_fusion.2), calls=%async_computation | async-start | bytes 4194304 | tf_op jit(solution)/shard_map/all_to_all | solution.py:106
  294.9 8.1 convert_bitcast_fusion.3
  303.0 4.1 copy.345
  308.2 15.7 %all-to-all-done = bf16[1,64,128,128]{3,2,0,1:T(8,128)(2,1)S(1)} async-done(((bf16[1,64,128,128]{3,2,0,1:T(8,128)(2,1)}), bf16[1,64,128,128]{3,2,0,1:T(8,128)(2,1)S(1)}, u32[]{:S(2)}, u32[]{:S(2)}) %all-to-all-start) | async-done | bytes 2097184 | tf_op jit(solution)/shard_map/all_to_all | solution.py:106
  326.0 4.8 pad_maximum_fusion
  330.8 10.1 %copy.346 = bf16[256,97,128]{2,1,0:T(8,128)(2,1)} copy(bf16[256,97,128]{0,2,1:T(8,128)(2,1)} %pad_maximum_fusion) | data formatting | bytes 12713984 | tf_op jit(solution)/shard_map/concatenate | solution.py:117
  340.9 13.5 %fusion.60 = f32[256,97,97]{2,1,0:T(8,128)} fusion(bf16[256,97,128]{2,1,0:T(8,128)(2,1)} %copy.346), kind=kOutput, calls=%fused_computation.184 | convolution fusion | flops 616628224 | bytes 15991808 | tf_op jit(solution)/shard_map/bie,bje->bij/dot_general | solution.py:118
  528.4 14.2 %concatenate.14 = f32[256,4656]{1,0:T(8,128)} concatenate(f32[256,1]{1,0:T(8,128)S(1)} %bitcast.539, f32[256,2]{1,0:T(8,128)S(1)} %bitcast.540, f32[256,3]{1,0:T(8,128)S(1)} %bitcast.541, f32[256,4]{1,0:T(8,128)S(1)} %bitcast.542, f32[256,5]{1,0:T(8,128)S(1)} %bitcast.543, f32[256,6]{1,0:T(8,128)S(1)} %bitcast.544, f32[256,7]{1,0:T(8,128)S(1)} %bitcast.545, ...), dimensions={1} | concatenate | bytes 9535488 | tf_op jit(solution)/shard_map/concatenate | solution.py:46
  545.6 6.2 multiply_reduce_fusion
  628.2 15.5 %copy.443 = f32[256,97,97]{1,0,2:T(8,128)} copy(f32[256,97,97]{2,0,1:T(8,128)} %constant_dynamic-update-slice_fusion) | data formatting | bytes 19269632 | tf_op jit(solution)/shard_map/stack | solution.py:56
  643.7 12.3 %bitcast_add_fusion = bf16[256,97,97]{2,0,1:T(8,128)(2,1)} fusion(f32[256,97,97]{2,0,1:T(8,128)} %constant_dynamic-update-slice_fusion, f32[256,97,97]{1,0,2:T(8,128)} %copy.443), kind=kLoop, calls=%fused_computation.7 | loop fusion | flops 4817408 | bytes 24087040 | tf_op jit(solution)/shard_map/add | solution.py:130
  656.1 12.3 %fusion.11 = bf16[256,97,128]{2,1,0:T(8,128)(2,1)} fusion(bf16[256,97,128]{2,1,0:T(8,128)(2,1)S(1)} %bitcast.528, bf16[256,97,97]{2,0,1:T(8,128)(2,1)} %bitcast_add_fusion), kind=kOutput, calls=%fused_computation.20 | convolution fusion | flops 616628224 | bytes 17531392 | tf_op jit(solution)/shard_map/bij,bje->bie/dot_general | solution.py:131
  671.3 6.3 fusion
  677.7 5.1 slice.982
  682.8 5.9 convert_bitcast_fusion.1
  688.7 4.7 all-to-all-start.1
  694.2 33.1 %all-to-all-done.1 = bf16[64,1,128,128]{3,2,1,0:T(8,128)(2,1)S(1)} async-done(((bf16[64,1,128,128]{3,2,1,0:T(8,128)(2,1)}), bf16[64,1,128,128]{3,2,1,0:T(8,128)(2,1)S(1)}, u32[]{:S(2)}, u32[]{:S(2)}) %all-to-all-start.1) | async-done | bytes 2097184 | tf_op jit(solution)/shard_map/all_to_all | solution.py:146
  727.2 5.0 fusion.17
  732.2 90.0 %scatter_custom_fusion = f32[8192,128]{1,0:T(8,128)} fusion(s32[16384]{0:T(1024)S(1)} %broadcast_select_fusion, f32[16384,128]{1,0:T(8,128)} %bitcast.529, f32[]{:T(128)} %constant.16.clone.1), kind=kCustom, calls=%fused_computation.43 | custom fusion | flops 2097152 | bytes 4194816
  822.3 3.7 convert_element_type.266
  826.0 75.3 %all-reduce.98.cloned.1.call-done = f32[32,512,128]{2,1,0:T(8,128)} async-done(((f32[32,512,128]{2,1,0:T(8,128)}), f32[32,512,128]{2,1,0:T(8,128)}) %all-reduce.98.cloned.1.call-update) | async-done | bytes 8388624 | tf_op jit(solution)/shard_map/psum | solution.py:140
  901.3 8.0 subtract_convert_fusion
  (355 shorter events, 268.1 us)
Async XLA Ops:
  8.0 299.2 %copy-start = (s32[64,128]{1,0:T(8,128)S(1)}, s32[64,128]{1,0:T(8,128)}, u32[]{:S(2)}) copy-start(s32[64,128]{1,0:T(8,128)} %param.16) | copy-start | bytes 98308
  9.6 267.6 %copy-start.4 = (s32[64,128]{1,0:T(8,128)}, s32[64,128]{1,0:T(8,128)S(1)}, u32[]{:S(2)}) copy-start(s32[64,128]{1,0:T(8,128)S(1)} %get-tuple-element.7) | copy-start | bytes 98308
  277.2 17.7 %copy-start.11 = (s32[256,32]{0,1:T(8,128)S(1)}, s32[256,32]{0,1:T(8,128)}, u32[]{:S(2)}) copy-start(s32[256,32]{0,1:T(8,128)} %param.12) | copy-start | bytes 98308
  283.5 23.6 %copy-start.6 = (bf16[256,128]{1,0:T(8,128)(2,1)S(1)}, bf16[256,128]{1,0:T(8,128)(2,1)}, u32[]{:S(2)}) copy-start(bf16[256,128]{1,0:T(8,128)(2,1)} %param.11) | copy-start | bytes 196612
  283.5 40.4 %all-to-all-start = ((bf16[1,64,128,128]{3,2,0,1:T(8,128)(2,1)}), bf16[1,64,128,128]{3,2,0,1:T(8,128)(2,1)S(1)}, u32[]{:S(2)}, u32[]{:S(2)}) async-start(bf16[1,64,128,128]{3,2,0,1:T(8,128)(2,1)} %convert_bitcast_fusion.2), calls=%async_computation | async-start | bytes 4194304 | tf_op jit(solution)/shard_map/all_to_all | solution.py:106
  294.5 606.7 %all-reduce.98.cloned.1.call-start = ((), (), s32[]{:S(2)}) async-start(), calls=%async_computation.2 | async-start | bytes 16777216 | tf_op jit(solution)/shard_map/psum | solution.py:140
  524.4 21.1 %copy-start.13 = (f32[1024]{0:T(1024)S(1)}, f32[1024]{0:T(1024)}, u32[]{:S(2)}) copy-start(f32[1024]{0:T(1024)} %param.20) | copy-start | bytes 12292
  524.4 21.1 %copy-start.14 = (f32[1024]{0:T(1024)S(1)}, f32[1024]{0:T(1024)}, u32[]{:S(2)}) copy-start(f32[1024]{0:T(1024)} %param.21) | copy-start | bytes 12292
  542.6 9.2 slice-start.2
  545.5 6.2 copy-start.7
  545.5 6.3 slice-start.3
  545.6 6.3 slice-start.4
  554.9 9.9 %copy-start.10 = (pred[97]{0:T(512)(128)(4,1)S(1)}, pred[97]{0:T(512)(128)(4,1)}, u32[]{:S(2)}) copy-start(pred[97]{0:T(512)(128)(4,1)} %constant.17.clone.1) | copy-start | bytes 295
  628.2 27.8 %slice-start = ((s8[6815744]{0:T(1024)(128)(4,1)}), s8[2621440]{0:T(1024)(128)(4,1)S(1)}, s32[]{:S(2)}) async-start(s8[6815744]{0:T(1024)(128)(4,1)} %bitcast.527), calls=%async_computation.4 | async-start | bytes 5242880
  643.7 12.3 %slice-start.1 = ((s8[6815744]{0:T(1024)(128)(4,1)}), s8[4194304]{0:T(1024)(128)(4,1)S(1)}, s32[]{:S(2)}) async-start(s8[6815744]{0:T(1024)(128)(4,1)} %bitcast.527), calls=%async_computation.5 | async-start | bytes 8388608
  656.1 15.2 %copy-start.12 = (s32[256,32]{0,1:T(8,128)S(1)}, s32[256,32]{0,1:T(8,128)}, u32[]{:S(2)}) copy-start(s32[256,32]{0,1:T(8,128)} %param.12) | copy-start | bytes 98308
  677.6 15.8 %copy-start.3 = (s32[1,64,256]{2,1,0:T(8,128)S(1)}, s32[1,64,256]{2,1,0:T(8,128)}, u32[]{:S(2)}) copy-start(s32[1,64,256]{2,1,0:T(8,128)} %get-tuple-element.3) | copy-start | bytes 196612
  677.6 15.9 %copy-start.9 = (s32[2]{0:T(128)S(1)}, s32[2]{0:T(128)}, u32[]{:S(2)}) copy-start(s32[2]{0:T(128)} %constant.246) | copy-start | bytes 28
  677.6 16.2 %copy-start.8 = (s32[2]{0:T(128)S(1)}, s32[2]{0:T(128)}, u32[]{:S(2)}) copy-start(s32[2]{0:T(128)} %constant.249) | copy-start | bytes 28
  677.7 49.6 %copy-start.5 = (s32[64,128]{1,0:T(8,128)S(1)}, s32[64,128]{1,0:T(8,128)}, u32[]{:S(2)}) copy-start(s32[64,128]{1,0:T(8,128)} %copy-done.4) | copy-start | bytes 98308
  688.7 38.5 %all-to-all-start.1 = ((bf16[64,1,128,128]{3,2,1,0:T(8,128)(2,1)}), bf16[64,1,128,128]{3,2,1,0:T(8,128)(2,1)S(1)}, u32[]{:S(2)}, u32[]{:S(2)}) async-start(bf16[64,1,128,128]{3,2,1,0:T(8,128)(2,1)} %convert_bitcast_fusion.1), calls=%async_computation.1 | async-start | bytes 4194304 | tf_op jit(solution)/shard_map/all_to_all | solution.py:146
  693.4 215.9 %all-gather.3.cloned.1.call-start = ((), (), s32[]{:S(2)}) async-start(), calls=%async_computation.3 | async-start | bytes 6291456 | tf_op jit(solution)/shard_map/all_gather | solution.py:18
  826.0 86.7 %copy-start.2 = (bf16[1,8192,128]{2,1,0:T(8,128)(2,1)S(1)}, bf16[1,8192,128]{2,1,0:T(8,128)(2,1)}, u32[]{:S(2)}) copy-start(bf16[1,8192,128]{2,1,0:T(8,128)(2,1)} %param.15) | copy-start | bytes 6291460
  826.0 88.7 %copy-start.1 = (s32[64,128]{1,0:T(8,128)S(1)}, s32[64,128]{1,0:T(8,128)}, u32[]{:S(2)}) copy-start(s32[64,128]{1,0:T(8,128)} %param.16) | copy-start | bytes 98308
Sparse Core Ops, SparseCore 0:
  677.7 223.4 all-reduce.97
Sparse Core Ops, SparseCore 1:
  826.1 61.7 all-gather.2
where the time goes:
time: 933 us; the launch traced here: 922 us
  local copies, waits for them, and re-layouts  566 us (61%)
  other arithmetic  130 us (14%)
  waiting for transfers between devices  124 us (13%)
  matrix products  68.6 us (7%)
  between operations  17 us (2%)
  starting transfers between devices  16.1 us (2%)
    gather x2, local copies, waits for them, and re-layouts, take_rows(): return table_one[row_list]  266 us
    slice x96, local copies, waits for them, and re-layouts, lower_pairs(): pieces = [gram_matrix[:, index, :index] for index in range(1, vec_count)]  174 us
    unnamed x8, other arithmetic  91.3 us
    psum x1, waiting for transfers between devices, shards(): small_sum = lax.psum(small_local, ('rep', 'shard'))  75.3 us
    unnamed x137, local copies, waits for them, and re-layouts  63 us
    all_to_all x1, waiting for transfers between devices, shards(): lax.all_to_all(folded[:, None], 'shard', split_axis=0, concat_axis=1, til...  33.1 us
  transfers between devices with their start and end apart: 4, of which 3 were waited for; matrix products, arithmetic and copies ran while one was open for 14% of the time, Pallas kernels for 0%

commit v1 on v0

--- a/solution.py
+++ b/solution.py
@@ -4,6 +4,12 @@
 from jax.sharding import PartitionSpec as P
 
 step_size = 32.0
+
+
+def series_supply(target):
+    for m in ("shard", "rep"):
+        target = lax.psum(target, m)
+    return target
 
 
 def as_sent(array):
@@ -137,7 +143,7 @@
         vec_grad[:, 1 : 1 + small_count],
         preferred_element_type=jnp.float32,
     )
-    small_sum = lax.psum(small_local, ("rep", "shard"))
+    small_sum = series_supply(small_local)
     small_new = (small_tables.astype(jnp.float32) - step_size * small_sum).astype(jnp.bfloat16)
     large_grad_part = vec_grad[:, 1 + small_count :]
     folded = jnp.einsum(

time: 933 us -> 1490 us (1.60)
  waiting for transfers between devices: 124 us -> 682 us
    psum x1 -> x2, waiting for transfers between devices: 75.3 us -> 634 us  [series_supply(): target = lax.psum(target, m)]
  transfers between devices with their start and end apart: 4 -> 5, of which waited for: 3 -> 4; matrix products, arithmetic and copies ran while one was open for 14% -> 9% of each run, Pallas kernels for 0% -> 0%
where the time goes in v1:
time: 1490 us; the launch traced here: 1480 us
  waiting for transfers between devices  682 us (46%)
  local copies, waits for them, and re-layouts  566 us (38%)
  other arithmetic  130 us (9%)
  matrix products  68.6 us (5%)
  between operations  17 us (1%)
  starting transfers between devices  16.2 us (1%)
    psum x2, waiting for transfers between devices, series_supply(): target = lax.psum(target, m)  634 us
    gather x2, local copies, waits for them, and re-layouts, take_rows(): return table_one[row_list]  266 us
    slice x96, local copies, waits for them, and re-layouts, lower_pairs(): pieces = [gram_matrix[:, index, :index] for index in range(1, vec_count)]  174 us
    unnamed x8, other arithmetic  91.3 us
    unnamed x137, local copies, waits for them, and re-layouts  63 us
    all_to_all x1, waiting for transfers between devices, shards(): lax.all_to_all(folded[:, None], 'shard', split_axis=0, concat_axis=1, til...  31.9 us
  transfers between devices with their start and end apart: 5, of which 4 were waited for; matrix products, arithmetic and copies ran while one was open for 9% of the time, Pallas kernels for 0%

profile of v1, /device:TPU:1, one launch (start us, length us, event | category | flops | bytes accessed | tf_op | source)
XLA Modules:
  0.0 1480.1 jit_solution(1628112282659745365)
XLA Ops:
  11.2 266.0 %gather_fusion = bf16[16384,128]{1,0:T(8,128)(2,1)} fusion(bf16[1,8192,128]{2,1,0:T(8,128)(2,1)} %param.15, s32[16384]{0:T(1024)S(1)} %bitcast.526), kind=kCustom, calls=%fused_computation | custom fusion | bytes 8519680 | tf_op jit(solution)/shard_map/vmap()/gather | solution.py:47
  277.2 6.3 convert_bitcast_fusion.2
  283.5 11.1 all-to-all-start
  294.9 8.1 convert_bitcast_fusion.3
  303.0 4.1 copy.345
  308.2 15.7 %all-to-all-done = bf16[1,64,128,128]{3,2,0,1:T(8,128)(2,1)S(1)} async-done(((bf16[1,64,128,128]{3,2,0,1:T(8,128)(2,1)}), bf16[1,64,128,128]{3,2,0,1:T(8,128)(2,1)S(1)}, u32[]{:S(2)}, u32[]{:S(2)}) %all-to-all-start) | async-done | bytes 2097184 | tf_op jit(solution)/shard_map/all_to_all | solution.py:112
  326.0 4.8 pad_maximum_fusion
  330.8 10.1 copy.346
  340.9 13.5 fusion.60
  528.4 14.2 concatenate.14
  545.6 6.2 multiply_reduce_fusion
  628.2 15.5 %copy.443 = f32[256,97,97]{1,0,2:T(8,128)} copy(f32[256,97,97]{2,0,1:T(8,128)} %constant_dynamic-update-slice_fusion) | data formatting | bytes 19269632 | tf_op jit(solution)/shard_map/stack | solution.py:62
  643.7 12.3 bitcast_add_fusion
  656.1 12.3 fusion.11
  671.3 6.3 fusion
  677.7 5.1 slice.982
  682.8 5.9 convert_bitcast_fusion.1
  688.7 4.7 all-to-all-start.1
  694.2 31.9 %all-to-all-done.1 = bf16[64,1,128,128]{3,2,1,0:T(8,128)(2,1)S(1)} async-done(((bf16[64,1,128,128]{3,2,1,0:T(8,128)(2,1)}), bf16[64,1,128,128]{3,2,1,0:T(8,128)(2,1)S(1)}, u32[]{:S(2)}, u32[]{:S(2)}) %all-to-all-start.1) | async-done | bytes 2097184 | tf_op jit(solution)/shard_map/all_to_all | solution.py:152
  726.1 5.0 fusion.17
  731.1 90.0 %scatter_custom_fusion = f32[8192,128]{1,0:T(8,128)} fusion(s32[16384]{0:T(1024)S(1)} %broadcast_select_fusion, f32[16384,128]{1,0:T(8,128)} %bitcast.529, f32[]{:T(128)} %constant.16.clone.1), kind=kCustom, calls=%fused_computation.43 | custom fusion | flops 2097152 | bytes 4194816
  825.0 433.2 %all-reduce.99.cloned.1.call-done = f32[32,512,128]{2,1,0:T(8,128)} async-done(((f32[32,512,128]{2,1,0:T(8,128)}), f32[32,512,128]{2,1,0:T(8,128)}) %all-reduce.99.cloned.1.call-update) | async-done | bytes 8388624 | tf_op jit(solution)/shard_map/psum | solution.py:11
  1263.7 200.8 %all-reduce.101.cloned.1.call-done = f32[32,512,128]{2,1,0:T(8,128)} async-done(((f32[32,512,128]{2,1,0:T(8,128)}), f32[32,512,128]{2,1,0:T(8,128)}) %all-reduce.101.cloned.1.call-update) | async-done | bytes 8388624 | tf_op jit(solution)/shard_map/psum | solution.py:11
  1464.5 8.0 subtract_convert_fusion
  (358 shorter events, 272.1 us)
Async XLA Ops:
  8.0 299.2 %copy-start = (s32[64,128]{1,0:T(8,128)S(1)}, s32[64,128]{1,0:T(8,128)}, u32[]{:S(2)}) copy-start(s32[64,128]{1,0:T(8,128)} %param.16) | copy-start | bytes 98308
  9.6 267.6 %copy-start.4 = (s32[64,128]{1,0:T(8,128)}, s32[64,128]{1,0:T(8,128)S(1)}, u32[]{:S(2)}) copy-start(s32[64,128]{1,0:T(8,128)S(1)} %get-tuple-element.7) | copy-start | bytes 98308
  277.2 17.7 %copy-start.11 = (s32[256,32]{0,1:T(8,128)S(1)}, s32[256,32]{0,1:T(8,128)}, u32[]{:S(2)}) copy-start(s32[256,32]{0,1:T(8,128)} %param.12) | copy-start | bytes 98308
  283.5 23.7 %copy-start.6 = (bf16[256,128]{1,0:T(8,128)(2,1)S(1)}, bf16[256,128]{1,0:T(8,128)(2,1)}, u32[]{:S(2)}) copy-start(bf16[256,128]{1,0:T(8,128)(2,1)} %param.11) | copy-start | bytes 196612
  283.5 40.4 %all-to-all-start = ((bf16[1,64,128,128]{3,2,0,1:T(8,128)(2,1)}), bf16[1,64,128,128]{3,2,0,1:T(8,128)(2,1)S(1)}, u32[]{:S(2)}, u32[]{:S(2)}) async-start(bf16[1,64,128,128]{3,2,0,1:T(8,128)(2,1)} %convert_bitcast_fusion.2), calls=%async_computation | async-start | bytes 4194304 | tf_op jit(solution)/shard_map/all_to_all | solution.py:112
  294.5 963.7 %all-reduce.99.cloned.1.call-start = ((), (), s32[]{:S(2)}) async-start(), calls=%async_computation.2 | async-start | bytes 16777216 | tf_op jit(solution)/shard_map/psum | solution.py:11
  524.4 21.1 %copy-start.13 = (f32[1024]{0:T(1024)S(1)}, f32[1024]{0:T(1024)}, u32[]{:S(2)}) copy-start(f32[1024]{0:T(1024)} %param.20) | copy-start | bytes 12292
  524.4 21.1 %copy-start.14 = (f32[1024]{0:T(1024)S(1)}, f32[1024]{0:T(1024)}, u32[]{:S(2)}) copy-start(f32[1024]{0:T(1024)} %param.21) | copy-start | bytes 12292
  542.6 9.2 slice-start.2
  545.5 6.3 slice-start.3
  545.6 6.3 slice-start.4
  554.9 9.9 copy-start.10
  628.2 27.8 %slice-start = ((s8[6815744]{0:T(1024)(128)(4,1)}), s8[2621440]{0:T(1024)(128)(4,1)S(1)}, s32[]{:S(2)}) async-start(s8[6815744]{0:T(1024)(128)(4,1)} %bitcast.527), calls=%async_computation.5 | async-start | bytes 5242880
  643.7 12.3 slice-start.1
  656.1 15.2 %copy-start.12 = (s32[256,32]{0,1:T(8,128)S(1)}, s32[256,32]{0,1:T(8,128)}, u32[]{:S(2)}) copy-start(s32[256,32]{0,1:T(8,128)} %param.12) | copy-start | bytes 98308
  677.6 15.8 %copy-start.3 = (s32[1,64,256]{2,1,0:T(8,128)S(1)}, s32[1,64,256]{2,1,0:T(8,128)}, u32[]{:S(2)}) copy-start(s32[1,64,256]{2,1,0:T(8,128)} %get-tuple-element.3) | copy-start | bytes 196612
  677.6 15.9 %copy-start.9 = (s32[2]{0:T(128)S(1)}, s32[2]{0:T(128)}, u32[]{:S(2)}) copy-start(s32[2]{0:T(128)} %constant.246) | copy-start | bytes 28
  677.6 16.2 %copy-start.8 = (s32[2]{0:T(128)S(1)}, s32[2]{0:T(128)}, u32[]{:S(2)}) copy-start(s32[2]{0:T(128)} %constant.249) | copy-start | bytes 28
  677.7 48.4 %copy-start.5 = (s32[64,128]{1,0:T(8,128)S(1)}, s32[64,128]{1,0:T(8,128)}, u32[]{:S(2)}) copy-start(s32[64,128]{1,0:T(8,128)} %copy-done.4) | copy-start | bytes 98308
  688.7 37.4 %all-to-all-start.1 = ((bf16[64,1,128,128]{3,2,1,0:T(8,128)(2,1)}), bf16[64,1,128,128]{3,2,1,0:T(8,128)(2,1)S(1)}, u32[]{:S(2)}, u32[]{:S(2)}) async-start(bf16[64,1,128,128]{3,2,1,0:T(8,128)(2,1)} %convert_bitcast_fusion.1), calls=%async_computation.1 | async-start | bytes 4194304 | tf_op jit(solution)/shard_map/all_to_all | solution.py:152
  693.4 564.9 %all-gather.3.cloned.1.call-start = ((), (), s32[]{:S(2)}) async-start(), calls=%async_computation.4 | async-start | bytes 6291456 | tf_op jit(solution)/shard_map/all_gather | solution.py:24
  821.1 440.6 %copy-start.2 = (bf16[1,8192,128]{2,1,0:T(8,128)(2,1)S(1)}, bf16[1,8192,128]{2,1,0:T(8,128)(2,1)}, u32[]{:S(2)}) copy-start(bf16[1,8192,128]{2,1,0:T(8,128)(2,1)} %param.15) | copy-start | bytes 6291460
  825.0 639.5 %all-reduce.101.cloned.1.call-start = ((), (), s32[]{:S(2)}) async-start(), calls=%async_computation.3 | async-start | bytes 16777216 | tf_op jit(solution)/shard_map/psum | solution.py:11
  1258.3 214.2 %copy-start.1 = (s32[64,128]{1,0:T(8,128)S(1)}, s32[64,128]{1,0:T(8,128)}, u32[]{:S(2)}) copy-start(s32[64,128]{1,0:T(8,128)} %param.16) | copy-start | bytes 98308
  (1 other events, 6.2 us)
Sparse Core Ops, SparseCore 0:
  677.7 580.4 all-reduce.98
Sparse Core Ops, SparseCore 1:
  825.1 67.9 all-gather.2
  1258.3 206.1 all-reduce.100
